TPU v7x, 32 devices: a whole 2x2x4 slice. The times are simulated.
32 devices in a mesh: rep: 1, ep: 16 (over z, y, x), sub: 2 (over core).
Axes of the slice: x: 2, y: 2, z: 4, core: 2. Of those that a mesh axis runs over, the one named last changes fastest.
Arguments:
- tokens: bfloat16 [256, 5120], P(('rep', 'ep'), 'sub'), may hold values from -6 to 6
- expert_ids: int32 [256, 1], P(('rep', 'ep')), may hold values from 0 to 1; in each aligned block of 16 rows (0 to 15, 16 to 31, ...) at most 16 rows name the same one
- router_score: float32 [256, 1], P(('rep', 'ep')), may hold values from -8 to 8
- expert_gate_up: bfloat16 [5120, 2, 8192], P('sub', None, 'ep'), may hold values from -0.078125 to 0.078125
- expert_down: bfloat16 [8192, 5120], P('ep', 'sub'), may hold values from -0.09375 to 0.09375
- shared_gate_up: bfloat16 [5120, 2, 8192], P('sub', None, 'ep'), may hold values from -0.078125 to 0.078125
- shared_down: bfloat16 [8192, 5120], P('ep', 'sub'), may hold values from -0.0625 to 0.0625
Outputs:
- mixed: bfloat16 [256, 5120], P(('rep', 'ep'), 'sub')
Inputs may be any that keep to these rules, and one draw needn't show every extreme that they name: `expert_ids`: in the rows of one index of ep (aligned blocks of 16 rows) no expert is named more than 16 times, a bound that some block reaches.
All inputs are finite; a program needn't handle non-finite values.
Results may differ from a plain program's by a relative error of at most 0.017.
Values may be sent and summed in bfloat16 or wider, within the bound.
A program may use at most 64 MiB of HBM per device.

v0:
```python
import functools
import jax
import jax.numpy as jnp
from jax import lax
from jax.experimental import pallas as pl
from jax.experimental.pallas import tpu as pltpu
from jax.sharding import PartitionSpec as P

EXP_ROWS = 8
GRID_ROWS = 16
META = 128
KCHUNKS = 4


def layer_kernel(
    zn, tokens_ref, ids_ref, score_ref, egu_ref, edn_ref, sgu_ref, sdn_ref, out_ref,
    x_ref, raw_ref, w_ref, dn_ref, gsend_ref, grecv_ref, hid_ref,
    sa1, ra1, sb1, rb1, sa2, ra2, sb2, rb2, acc_ref, zsend, zright, zleft,
    wsem, dsem, ag_send, ag_recv_a, ag_recv_b, g_send, g_recv,
    xy_send, xy_recv, z_send, zr_recv, zl_recv,
):
    tr, half = tokens_ref.shape
    hidden = edn_ref.shape[0]
    line = zn * tr
    hw = hidden // 2
    cut = half // 2
    kc = half // KCHUNKS
    rep = lax.axis_index("rep")
    sub = lax.axis_index("sub")
    me = lax.axis_index("ep")
    z = me // 4
    y = (me // 2) % 2
    x = me % 2

    def at(ep, s=None):
        return (rep, ep, sub if s is None else s)

    xn = at(z * 4 + y * 2 + (1 - x))
    yn = at(z * 4 + (1 - y) * 2 + x)
    up = at(jnp.minimum(z + 1, zn - 1) * 4 + y * 2 + x)
    down = at(jnp.maximum(z - 1, 0) * 4 + y * 2 + x)
    partner = at(me, 1 - sub)
    mesh_id = pl.DeviceIdType.MESH

    loads = []
    for m, src in enumerate((egu_ref, sgu_ref)):
        for k in range(KCHUNKS):
            c = pltpu.make_async_copy(
                src.at[pl.ds(k * kc, kc)], raw_ref.at[m, pl.ds(k * kc, kc)], wsem.at[m, k]
            )
            c.start()
            loads.append((m, k, c))
    dloads = []
    for m, src in enumerate((edn_ref, sdn_ref)):
        c = pltpu.make_async_copy(src, dn_ref.at[pl.ds(m * hidden, hidden)], dsem.at[m])
        c.start()
        dloads.append(c)

    eye = lax.broadcasted_iota(jnp.int32, (tr, tr), 0) == lax.broadcasted_iota(
        jnp.int32, (tr, tr), 1
    )
    gate_row = 1.0 / (1.0 + jnp.exp(-score_ref[...]))
    id_row = ids_ref[...].astype(jnp.float32)
    gate_col = jnp.sum(jnp.where(eye, gate_row, 0.0), axis=1, keepdims=True)
    id_col = jnp.sum(jnp.where(eye, id_row, 0.0), axis=1, keepdims=True)
    gate_hi = gate_col.astype(jnp.bfloat16).astype(jnp.float32)
    lane = lax.broadcasted_iota(jnp.int32, (tr, META), 1)
    meta = jnp.where(
        lane == 0, gate_hi, jnp.where(lane == 1, gate_col - gate_hi, jnp.where(lane == 2, id_col, 0.0))
    )
    own = pl.ds(pl.multiple_of(z * tr, tr), tr)
    x_ref[own, 0:half] = tokens_ref[...]
    x_ref[own, half:] = meta.astype(jnp.bfloat16)

    barrier = pltpu.get_barrier_semaphore()
    for nb in (xn, yn, partner):
        pl.semaphore_signal(barrier, inc=1, device_id=nb, device_id_type=mesh_id)

    @pl.when(z < zn - 1)
    def _():
        pl.semaphore_signal(barrier, inc=1, device_id=up, device_id_type=mesh_id)

    @pl.when(z > 0)
    def _():
        pl.semaphore_signal(barrier, inc=1, device_id=down, device_id_type=mesh_id)

    pl.semaphore_wait(
        barrier, 3 + (z < zn - 1).astype(jnp.int32) + (z > 0).astype(jnp.int32)
    )

    def rows_of(xr, yr, b):
        return pl.ds(pl.multiple_of(((xr * 2 + yr) * zn + b) * tr, tr), tr)

    wide_a, wide_b = pl.ds(0, cut), pl.ds(cut, half + META - cut)

    def copy(src_slot, dst_slot, cols, kind, b, recv, dev):
        return pltpu.make_async_remote_copy(
            src_ref=x_ref.at[rows_of(*src_slot), cols],
            dst_ref=x_ref.at[rows_of(*dst_slot), cols],
            send_sem=ag_send.at[kind, b],
            recv_sem=recv.at[(dst_slot[0] * 2 + dst_slot[1]) * zn + dst_slot[2]],
            device_id=dev, device_id_type=mesh_id,
        )

    def c_up(h, b):
        return copy((0, 0, b), (0, 0, b), (wide_a, wide_b)[h], 8 * h, b, (ag_recv_a, ag_recv_b)[h], up)

    def c_down(h, b):
        return copy((0, 0, b), (0, 0, b), (wide_a, wide_b)[h], 8 * h + 1, b, (ag_recv_a, ag_recv_b)[h], down)

    def c_ay(b):
        return copy((0, 0, b), (0, 1, b), wide_a, 2, b, ag_recv_a, yn)

    def c_ax(yr, b):
        return copy((0, yr, b), (1, yr, b), wide_a, 3 + yr, b, ag_recv_a, xn)

    def c_bx(b):
        return copy((0, 0, b), (1, 0, b), wide_b, 5, b, ag_recv_b, xn)

    def c_by(xr, b):
        return copy((xr, 0, b), (xr, 1, b), wide_b, 6 + xr, b, ag_recv_b, yn)

    def spread(h, b):
        if h == 0:
            c_ay(b).start()
            c_ax(0, b).start()
        else:
            c_bx(b).start()
            c_by(0, b).start()

    def relay(b):
        c_ay(b).wait_recv()
        c_ax(1, b).start()
        c_bx(b).wait_recv()
        c_by(1, b).start()

    pending = list(loads)

    def deinterleave(count):
        for _ in range(min(count, len(pending))):
            m, k, c = pending.pop(0)
            c.wait()
            step = 128 if kc % 128 == 0 else kc

            @pl.loop(0, kc // step)
            def _(i):
                s = pl.ds(pl.multiple_of(k * kc + i * step, step), step)
                w_ref[s, m * 2 * hidden:(m + 1) * 2 * hidden] = raw_ref[m, s].reshape(
                    step, 2 * hidden
                )

    for h in range(2):
        @pl.when(z < zn - 1)
        def _():
            c_up(h, z).start()

        @pl.when(z > 0)
        def _():
            c_down(h, z).start()

    c_ay(z).start()
    c_bx(z).start()
    c_ax(0, z).start()
    c_by(0, z).start()
    for s in range(1, zn):
        for h in range(2):
            @pl.when(z - s >= 0)
            def _():
                b = jnp.maximum(z - s, 0)
                c_up(h, b).wait_recv()

                @pl.when(z < zn - 1)
                def _():
                    c_up(h, b).start()

                spread(h, b)

            @pl.when(z + s <= zn - 1)
            def _():
                b = jnp.minimum(z + s, zn - 1)
                c_down(h, b).wait_recv()

                @pl.when(z > 0)
                def _():
                    c_down(h, b).start()

                spread(h, b)

        if s == 1:
            relay(z)
        else:
            @pl.when(z - s + 1 >= 0)
            def _():
                relay(jnp.maximum(z - s + 1, 0))

            @pl.when(z + s - 1 <= zn - 1)
            def _():
                relay(jnp.minimum(z + s - 1, zn - 1))

        if s < zn - 1:
            deinterleave(3)

    @pl.when(z - zn + 1 >= 0)
    def _():
        relay(jnp.maximum(z - zn + 1, 0))

    @pl.when(z + zn - 1 <= zn - 1)
    def _():
        relay(jnp.minimum(z + zn - 1, zn - 1))

    deinterleave(len(loads))
    quarter = 2 * line

    def c_g(r, i):
        part = pl.ds(r * quarter, quarter)
        return pltpu.make_async_remote_copy(
            src_ref=gsend_ref.at[i, part], dst_ref=grecv_ref.at[i, part],
            send_sem=g_send.at[r, i], recv_sem=g_recv.at[r, i],
            device_id=partner, device_id_type=mesh_id,
        )

    def hidden_of(r, i, scale):
        c_g(r, i).wait_recv()
        part = pl.ds(r * quarter, quarter)
        total = gsend_ref[i, part].astype(jnp.float32) + grecv_ref[i, part].astype(jnp.float32)
        if i < 2:
            total = total * scale
        g, u = total[:, :hw], total[:, hw:]
        hid_ref[part, i * hw:(i + 1) * hw] = (g / (1.0 + jnp.exp(-g)) * u).astype(jnp.bfloat16)

    own_expert = (me // EXP_ROWS).astype(jnp.float32)
    waiting = []
    for r in range(2):
        for b in range(zn):
            if r == 0:
                c_by(0, b).wait_recv()
            else:
                c_ax(0, b).wait_recv()
                c_ax(1, b).wait_recv()
                c_by(1, b).wait_recv()
        part = pl.ds(r * quarter, quarter)
        info = x_ref[part, half:].astype(jnp.float32)
        scale = jnp.where(info[:, 2:3] == own_expert, info[:, 0:1] + info[:, 1:2], 0.0)
        for i in range(4):
            base = (i // 2) * 2 * hidden + (i % 2) * hw
            for p in range(2):
                cols = slice(base + p * hidden, base + p * hidden + hw)
                gsend_ref[i, part, p * hw:(p + 1) * hw] = jnp.dot(
                    x_ref[part, :half], w_ref[:, cols], preferred_element_type=jnp.float32
                ).astype(jnp.bfloat16)
            c_g(r, i).start()
            if waiting:
                hidden_of(*waiting.pop(0))
            waiting.append((r, i, scale))
    hidden_of(*waiting.pop(0))
    for c in dloads:
        c.wait()

    def product(first, rows, col):
        return jnp.dot(
            hid_ref[pl.ds(first, rows), :], dn_ref[:, pl.ds(col, 256)],
            preferred_element_type=jnp.float32,
        )

    tiles = cut // 256

    def fill(dst, dst_row, first, rows, col0):
        @pl.loop(0, tiles)
        def _(t):
            off = pl.multiple_of(t * 256, 256)
            dst[pl.ds(dst_row, rows), pl.ds(off, 256)] = product(
                first, rows, pl.multiple_of(col0 + off, 256)
            ).astype(dst.dtype)

    def fill_acc(first, rows, col0):
        @pl.loop(0, tiles)
        def _(t):
            off = pl.multiple_of(col0 + t * 256, 256)
            acc_ref[pl.ds(first, rows), pl.ds(off, 256)] = product(first, rows, off)

    def block(b):
        return pl.ds(pl.multiple_of(b * tr, tr), tr)

    def c_xy(kind, d):
        src, dst, dev = ((sa1, ra1, xn), (sb1, rb1, yn), (sa2, ra2, yn), (sb2, rb2, xn))[kind % 4]
        rows = pl.ds(pl.multiple_of((line if kind >= 4 else 0) + d * tr, tr), tr)
        return pltpu.make_async_remote_copy(
            src_ref=src.at[rows], dst_ref=dst.at[rows],
            send_sem=xy_send.at[kind, d], recv_sem=xy_recv.at[kind, d],
            device_id=dev, device_id_type=mesh_id,
        )

    order = (3 - 3 * (z // 2), 2 * (1 - z % 2) + z // 2, 1 + z % 2, z)

    fill(sa1, 0, 2 * line, 2 * line, 0)
    for k in range(2):
        c_xy(4, order[k]).start()
        c_xy(0, order[k]).start()
    fill(sb1, line, 3 * line, line, cut)
    fill(sb1, 0, line, line, cut)
    for k in range(2):
        c_xy(5, order[k]).start()
        c_xy(1, order[k]).start()
    fill_acc(0, 2 * line, 0)
    fill_acc(2 * line, line, cut)
    fill_acc(0, line, cut)

    def shifted(base, d):
        return pl.ds(pl.multiple_of(base + d * tr, tr), tr)

    def second(d):
        c_xy(4, d).wait_recv()
        sa2[block(d), :] = (
            acc_ref[shifted(line, d), 0:cut] + ra1[shifted(line, d), :].astype(jnp.float32)
        ).astype(jnp.bfloat16)
        c_xy(2, d).start()
        c_xy(5, d).wait_recv()
        sb2[block(d), :] = (
            acc_ref[shifted(2 * line, d), cut:] + rb1[shifted(line, d), :].astype(jnp.float32)
        ).astype(jnp.bfloat16)
        c_xy(3, d).start()

    def settle(d):
        c_xy(0, d).wait_recv()
        c_xy(2, d).wait_recv()
        acc_ref[block(d), 0:cut] += ra1[block(d), :].astype(jnp.float32) + ra2[
            block(d), :
        ].astype(jnp.float32)
        c_xy(1, d).wait_recv()
        c_xy(3, d).wait_recv()
        acc_ref[block(d), cut:] += rb1[block(d), :].astype(jnp.float32) + rb2[
            block(d), :
        ].astype(jnp.float32)

    def c_zr(h, d):
        cols = pl.ds(h * cut, cut)
        return pltpu.make_async_remote_copy(
            src_ref=zsend.at[block(d), cols], dst_ref=zright.at[block(d), cols],
            send_sem=z_send.at[h, d], recv_sem=zr_recv.at[h, d],
            device_id=up, device_id_type=mesh_id,
        )

    def c_zl(h, d):
        cols = pl.ds(h * cut, cut)
        return pltpu.make_async_remote_copy(
            src_ref=zsend.at[block(d), cols], dst_ref=zleft.at[block(d), cols],
            send_sem=z_send.at[h, d], recv_sem=zl_recv.at[h, d],
            device_id=down, device_id_type=mesh_id,
        )

    def push(h, d, make, buf, has_source):
        cols = slice(h * cut, (h + 1) * cut)

        @pl.when(has_source)
        def _():
            make(h, d).wait_recv()
            zsend[block(d), cols] = (
                acc_ref[block(d), cols] + buf[block(d), cols].astype(jnp.float32)
            ).astype(jnp.bfloat16)

        @pl.when(jnp.logical_not(has_source))
        def _():
            zsend[block(d), cols] = acc_ref[block(d), cols].astype(jnp.bfloat16)

        make(h, d).start()

    def along(d):
        for h in range(2):
            @pl.when(d > z)
            def _():
                push(h, d, c_zr, zright, z > 0)

            @pl.when(d < z)
            def _():
                push(h, d, c_zl, zleft, z < zn - 1)

    for k in range(zn):
        second(order[k])
        if k + 2 < zn:
            for kind in (4, 0, 5, 1):
                c_xy(kind, order[k + 2]).start()
        if k > 0:
            settle(order[k - 1])
            along(order[k - 1])
    settle(z)

    for h in range(2):
        cols = slice(h * cut, (h + 1) * cut)

        @pl.when(z > 0)
        def _():
            c_zr(h, z).wait_recv()
            acc_ref[own, cols] += zright[own, cols].astype(jnp.float32)

        @pl.when(z < zn - 1)
        def _():
            c_zl(h, z).wait_recv()
            acc_ref[own, cols] += zleft[own, cols].astype(jnp.float32)

        out_ref[:, cols] = acc_ref[own, cols].astype(out_ref.dtype)

    for b in range(zn):
        for h in range(2):
            @pl.when(jnp.logical_and(z < zn - 1, b <= z))
            def _():
                c_up(h, b).wait_send()

            @pl.when(jnp.logical_and(z > 0, b >= z))
            def _():
                c_down(h, b).wait_send()

        for c in (c_ay(b), c_ax(0, b), c_ax(1, b), c_bx(b), c_by(0, b), c_by(1, b)):
            c.wait_send()
        for h in range(2):
            @pl.when(b != z)
            def _():
                c_zr(h, b).wait_send()
        for kind in range(6):
            c_xy(kind, b).wait_send()
    for r in range(2):
        for i in range(4):
            c_g(r, i).wait_send()


def fused_local(
    tokens, expert_ids, router_score, expert_gate_up, expert_down, shared_gate_up, shared_down
):
    tr, half = tokens.shape
    n = lax.axis_size("ep")
    zn = n // 4
    hidden = expert_down.shape[0]
    rows = n * tr
    line = zn * tr
    cut = half // 2
    bf, f32 = jnp.bfloat16, jnp.float32
    vm = pl.BlockSpec(memory_space=pltpu.VMEM)
    hbm = pl.BlockSpec(memory_space=pltpu.HBM)
    dma = pltpu.SemaphoreType.DMA
    return pl.pallas_call(
        functools.partial(layer_kernel, zn),
        out_shape=jax.ShapeDtypeStruct((tr, half), bf),
        in_specs=[vm, vm, vm, hbm, hbm, hbm, hbm],
        out_specs=vm,
        scratch_shapes=[
            pltpu.VMEM((rows, half + META), bf),
            pltpu.VMEM((2, half, 2, hidden), bf),
            pltpu.VMEM((half, 4 * hidden), bf),
            pltpu.VMEM((2 * hidden, half), bf),
            pltpu.VMEM((4, rows, hidden), bf),
            pltpu.VMEM((4, rows, hidden), bf),
            pltpu.VMEM((rows, 2 * hidden), bf),
            pltpu.VMEM((2 * line, cut), bf), pltpu.VMEM((2 * line, cut), bf),
            pltpu.VMEM((2 * line, cut), bf), pltpu.VMEM((2 * line, cut), bf),
            pltpu.VMEM((line, cut), bf), pltpu.VMEM((line, cut), bf),
            pltpu.VMEM((line, cut), bf), pltpu.VMEM((line, cut), bf),
            pltpu.VMEM((rows, half), f32),
            pltpu.VMEM((line, half), bf), pltpu.VMEM((line, half), bf), pltpu.VMEM((line, half), bf),
            dma((2, KCHUNKS)), dma((2,)), dma((10, zn)), dma((n,)), dma((n,)), dma((2, 4)), dma((2, 4)),
            dma((6, zn)), dma((6, zn)), dma((2, zn)), dma((2, zn)), dma((2, zn)),
        ],
        compiler_params=pltpu.CompilerParams(
            collective_id=0, has_side_effects=True, vmem_limit_bytes=56 * 2**20
        ),
    )(
        tokens, expert_ids.reshape(1, tr), router_score.reshape(1, tr),
        expert_gate_up, expert_down, shared_gate_up, shared_down,
    )


def slot_ranks(token_ids, experts):
    onehot = (token_ids[..., None] == jnp.arange(experts, dtype=jnp.int32)).astype(jnp.int32)
    before = jnp.cumsum(onehot, axis=-2) - onehot
    return jnp.sum(before * onehot, axis=-1)


def local_mlp(slot_rows, expert_gate_up, expert_down):
    hidden_width = expert_down.shape[0]
    gate_cols = expert_gate_up.reshape(expert_gate_up.shape[0], 2 * hidden_width)
    gate_up_sum = jnp.dot(slot_rows, gate_cols, preferred_element_type=jnp.float32)
    gate_up_sum = lax.psum(gate_up_sum.astype(jnp.bfloat16), "sub").astype(jnp.float32)
    gate_up_sum = gate_up_sum.reshape(slot_rows.shape[0], 2, hidden_width)
    hidden = (jax.nn.silu(gate_up_sum[:, 0]) * gate_up_sum[:, 1]).astype(jnp.bfloat16)
    return jnp.dot(hidden, expert_down, preferred_element_type=jnp.float32).astype(jnp.bfloat16)


def local(
    tokens, expert_ids, router_score, expert_gate_up, expert_down, shared_gate_up, shared_down
):
    rows_here, half_width = tokens.shape
    rows_ep = lax.axis_size("ep")
    experts = rows_ep // EXP_ROWS
    capacity = min(rows_here, max(2, 3 * rows_here // experts))
    shared_width = shared_down.shape[0]
    shared_in = shared_gate_up.reshape(half_width, 2 * shared_width)
    routed_extra = None
    all_tokens, all_ids, all_scores = (
        lax.all_gather(tokens, "ep", axis=0, tiled=True),
        lax.all_gather(expert_ids, "ep", axis=0, tiled=True),
        lax.all_gather(router_score.astype(jnp.bfloat16), "ep", axis=0, tiled=True).astype(
            router_score.dtype
        ),
    )
    shared_sum = jnp.dot(all_tokens, shared_in, preferred_element_type=jnp.float32)
    token_ids = all_ids[:, 0].reshape(rows_ep, rows_here)
    position = slot_ranks(token_ids, experts)
    own_expert = lax.axis_index("ep") // EXP_ROWS
    row_index = lax.broadcasted_iota(jnp.int32, (rows_ep, rows_here), 0)
    slot_index = jnp.where(token_ids == own_expert, row_index * capacity + position, -1).reshape(-1)
    slot_iota = lax.broadcasted_iota(jnp.int32, (rows_ep * capacity, rows_ep * rows_here), 0)
    select = (slot_iota == slot_index[None, :]).astype(jnp.bfloat16)
    weighted = (jax.nn.sigmoid(all_scores) * all_tokens.astype(jnp.float32)).astype(jnp.bfloat16)
    slot_rows = jnp.dot(select, weighted, preferred_element_type=jnp.float32).astype(jnp.bfloat16)
    results = local_mlp(slot_rows, expert_gate_up, expert_down)
    routed_extra = lax.dot_general(
        select, results, (((0,), (0,)), ((), ())), preferred_element_type=jnp.float32
    )
    shared_sum = lax.psum(shared_sum.astype(jnp.bfloat16), "sub").astype(jnp.float32)
    shared_sum = shared_sum.reshape(-1, 2, shared_width)
    shared_hidden = (jax.nn.silu(shared_sum[:, 0]) * shared_sum[:, 1]).astype(jnp.bfloat16)
    partial_value = jnp.dot(shared_hidden, shared_down, preferred_element_type=jnp.float32)
    partial_value = partial_value + routed_extra
    mixed = lax.psum_scatter(partial_value, "ep", scatter_dimension=0, tiled=True)
    return mixed.astype(jnp.bfloat16)


def solution(mesh):
    placed = (
        P(("rep", "ep"), "sub"),
        P(("rep", "ep"), None),
        P(("rep", "ep"), None),
        P("sub", None, "ep"),
        P("ep", "sub"),
        P("sub", None, "ep"),
        P("ep", "sub"),
    )
    fused = mesh.shape["ep"] == GRID_ROWS
    return jax.shard_map(
        fused_local if fused else local, mesh=mesh, in_specs=placed, out_specs=P(("rep", "ep"), "sub"), check_vma=False
    )
```

profile of v0, /device:TPU:0, one launch (start us, length us, event | category | flops | bytes accessed | tf_op | source)
XLA Modules:
  0.0 50.8 jit_solution(3880079006104772024)
XLA Ops:
  0.0 49.3 %shard_map.73 = bf16[16,2560]{1,0:T(8,128)(2,1)} custom-call(bf16[16,2560]{1,0:T(8,128)(2,1)} %tokens_ref.1, s32[1,16]{1,0:T(1,128)} %bitcast.2, f32[1,16]{1,0:T(1,128)} %bitcast.3, bf16[2560,2,512]{2,1,0:T(2,128)(2,1)} %egu_ref.1, bf16[512,2560]{1,0:T(8,128)(2,1)} %edn_ref.1, bf16[2560,2,512]{2,1,0:T(2,128)(2,1)} %sgu_ref.1, bf16[512,2560]{1,0:T(8,128)(2,1)} %sdn_ref.1), custom_call_target="tpu_custom_call" | custom-call | tf_op jit(solution)/shard_map/pallas_call | solution.py:439
  49.3 1.5 %copy.9 = bf16[16,2560]{1,0:T(8,128)(2,1)} copy(bf16[16,2560]{1,0:T(8,128)(2,1)} %shard_map.73) | data formatting | bytes 163840
where the time goes:
time: 51 us; the launch traced here: 50.8 us
  Pallas kernels  49.3 us (97%)
  local copies, waits for them, and re-layouts  1.53 us (3%)
    pallas_call x1, Pallas kernels, fused_local(): pl.pallas_call(functools.partial(layer_kernel, zn), out_shape=jax.ShapeDt...  49.3 us
    unnamed x1, local copies, waits for them, and re-layouts  1.53 us

commit v1 on v0

--- a/solution.py
+++ b/solution.py
@@ -15,9 +15,9 @@
 def layer_kernel(
     zn, tokens_ref, ids_ref, score_ref, egu_ref, edn_ref, sgu_ref, sdn_ref, out_ref,
     x_ref, raw_ref, w_ref, dn_ref, gsend_ref, grecv_ref, hid_ref,
-    sa1, ra1, sb1, rb1, sa2, ra2, sb2, rb2, acc_ref, zsend, zright, zleft,
-    wsem, dsem, ag_send, ag_recv_a, ag_recv_b, g_send, g_recv,
-    xy_send, xy_recv, z_send, zr_recv, zl_recv,
+    sa1, ra1, sb1, rb1, sa2, ra2, sb2, rb2, acc_ref, zsend, zrecv, id_v, score_v,
+    isem, wsem, dsem, ag_send, ag_recv_a, ag_recv_b, g_send, g_recv,
+    xy_send, xy_recv, z_send, z_recv,
 ):
     tr, half = tokens_ref.shape
     hidden = edn_ref.shape[0]
@@ -42,6 +42,27 @@
     partner = at(me, 1 - sub)
     mesh_id = pl.DeviceIdType.MESH
 
+    own = pl.ds(pl.multiple_of(z * tr, tr), tr)
+    inputs = [
+        pltpu.make_async_copy(tokens_ref, x_ref.at[own, pl.ds(0, half)], isem.at[0]),
+        pltpu.make_async_copy(ids_ref, id_v, isem.at[1]),
+        pltpu.make_async_copy(score_ref, score_v, isem.at[2]),
+    ]
+    for c in inputs:
+        c.start()
+
+    barrier = pltpu.get_barrier_semaphore()
+    for nb in (xn, yn, partner):
+        pl.semaphore_signal(barrier, inc=1, device_id=nb, device_id_type=mesh_id)
+
+    @pl.when(z < zn - 1)
+    def _():
+        pl.semaphore_signal(barrier, inc=1, device_id=up, device_id_type=mesh_id)
+
+    @pl.when(z > 0)
+    def _():
+        pl.semaphore_signal(barrier, inc=1, device_id=down, device_id_type=mesh_id)
+
     loads = []
     for m, src in enumerate((egu_ref, sgu_ref)):
         for k in range(KCHUNKS):
@@ -59,8 +80,10 @@
     eye = lax.broadcasted_iota(jnp.int32, (tr, tr), 0) == lax.broadcasted_iota(
         jnp.int32, (tr, tr), 1
     )
-    gate_row = 1.0 / (1.0 + jnp.exp(-score_ref[...]))
-    id_row = ids_ref[...].astype(jnp.float32)
+    for c in inputs:
+        c.wait()
+    gate_row = 1.0 / (1.0 + jnp.exp(-score_v[...]))
+    id_row = id_v[...].astype(jnp.float32)
     gate_col = jnp.sum(jnp.where(eye, gate_row, 0.0), axis=1, keepdims=True)
     id_col = jnp.sum(jnp.where(eye, id_row, 0.0), axis=1, keepdims=True)
     gate_hi = gate_col.astype(jnp.bfloat16).astype(jnp.float32)
@@ -68,21 +91,7 @@
     meta = jnp.where(
         lane == 0, gate_hi, jnp.where(lane == 1, gate_col - gate_hi, jnp.where(lane == 2, id_col, 0.0))
     )
-    own = pl.ds(pl.multiple_of(z * tr, tr), tr)
-    x_ref[own, 0:half] = tokens_ref[...]
     x_ref[own, half:] = meta.astype(jnp.bfloat16)
-
-    barrier = pltpu.get_barrier_semaphore()
-    for nb in (xn, yn, partner):
-        pl.semaphore_signal(barrier, inc=1, device_id=nb, device_id_type=mesh_id)
-
-    @pl.when(z < zn - 1)
-    def _():
-        pl.semaphore_signal(barrier, inc=1, device_id=up, device_id_type=mesh_id)
-
-    @pl.when(z > 0)
-    def _():
-        pl.semaphore_signal(barrier, inc=1, device_id=down, device_id_type=mesh_id)
 
     pl.semaphore_wait(
         barrier, 3 + (z < zn - 1).astype(jnp.int32) + (z > 0).astype(jnp.int32)
@@ -145,9 +154,11 @@
             @pl.loop(0, kc // step)
             def _(i):
                 s = pl.ds(pl.multiple_of(k * kc + i * step, step), step)
-                w_ref[s, m * 2 * hidden:(m + 1) * 2 * hidden] = raw_ref[m, s].reshape(
-                    step, 2 * hidden
-                )
+                pair = raw_ref[m, s].reshape(step, 2 * hidden)
+                for j in range(2):
+                    for p in range(2):
+                        to = (m * 2 + j) * hidden + p * hw
+                        w_ref[s, to:to + hw] = pair[:, p * hidden + j * hw:p * hidden + (j + 1) * hw]
 
     for h in range(2):
         @pl.when(z < zn - 1)
@@ -162,6 +173,7 @@
     c_bx(z).start()
     c_ax(0, z).start()
     c_by(0, z).start()
+    deinterleave(4)
     for s in range(1, zn):
         for h in range(2):
             @pl.when(z - s >= 0)
@@ -198,85 +210,65 @@
                 relay(jnp.minimum(z + s - 1, zn - 1))
 
         if s < zn - 1:
-            deinterleave(3)
-
-    @pl.when(z - zn + 1 >= 0)
-    def _():
-        relay(jnp.maximum(z - zn + 1, 0))
-
-    @pl.when(z + zn - 1 <= zn - 1)
-    def _():
-        relay(jnp.minimum(z + zn - 1, zn - 1))
+            deinterleave(2)
 
     deinterleave(len(loads))
-    quarter = 2 * line
+    groups = ((0, line), (line, 2 * line), (3 * line, line))
 
     def c_g(r, i):
-        part = pl.ds(r * quarter, quarter)
+        part = pl.ds(*groups[r])
         return pltpu.make_async_remote_copy(
             src_ref=gsend_ref.at[i, part], dst_ref=grecv_ref.at[i, part],
             send_sem=g_send.at[r, i], recv_sem=g_recv.at[r, i],
             device_id=partner, device_id_type=mesh_id,
         )
 
-    def hidden_of(r, i, scale):
-        c_g(r, i).wait_recv()
-        part = pl.ds(r * quarter, quarter)
-        total = gsend_ref[i, part].astype(jnp.float32) + grecv_ref[i, part].astype(jnp.float32)
-        if i < 2:
-            total = total * scale
-        g, u = total[:, :hw], total[:, hw:]
-        hid_ref[part, i * hw:(i + 1) * hw] = (g / (1.0 + jnp.exp(-g)) * u).astype(jnp.bfloat16)
+    def gate_up(r):
+        part = pl.ds(*groups[r])
+        for i in range(4):
+            gsend_ref[i, part] = jnp.dot(
+                x_ref[part, :half], w_ref[:, i * hidden:(i + 1) * hidden],
+                preferred_element_type=jnp.float32,
+            ).astype(jnp.bfloat16)
+            c_g(r, i).start()
 
     own_expert = (me // EXP_ROWS).astype(jnp.float32)
-    waiting = []
-    for r in range(2):
-        for b in range(zn):
-            if r == 0:
-                c_by(0, b).wait_recv()
-            else:
-                c_ax(0, b).wait_recv()
-                c_ax(1, b).wait_recv()
-                c_by(1, b).wait_recv()
-        part = pl.ds(r * quarter, quarter)
+
+    def activate(r):
+        part = pl.ds(*groups[r])
         info = x_ref[part, half:].astype(jnp.float32)
         scale = jnp.where(info[:, 2:3] == own_expert, info[:, 0:1] + info[:, 1:2], 0.0)
         for i in range(4):
-            base = (i // 2) * 2 * hidden + (i % 2) * hw
-            for p in range(2):
-                cols = slice(base + p * hidden, base + p * hidden + hw)
-                gsend_ref[i, part, p * hw:(p + 1) * hw] = jnp.dot(
-                    x_ref[part, :half], w_ref[:, cols], preferred_element_type=jnp.float32
-                ).astype(jnp.bfloat16)
-            c_g(r, i).start()
-            if waiting:
-                hidden_of(*waiting.pop(0))
-            waiting.append((r, i, scale))
-    hidden_of(*waiting.pop(0))
+            c_g(r, i).wait_recv()
+            total = gsend_ref[i, part].astype(jnp.float32) + grecv_ref[i, part].astype(jnp.float32)
+            if i < 2:
+                total = total * scale
+            g, u = total[:, :hw], total[:, hw:]
+            hid_ref[part, i * hw:(i + 1) * hw] = (g / (1.0 + jnp.exp(-g)) * u).astype(jnp.bfloat16)
+
+    gate_up(0)
+
+    @pl.when(z - zn + 1 >= 0)
+    def _():
+        relay(jnp.maximum(z - zn + 1, 0))
+
+    @pl.when(z + zn - 1 <= zn - 1)
+    def _():
+        relay(jnp.minimum(z + zn - 1, zn - 1))
+
+    activate(0)
+    for b in range(zn):
+        c_ax(0, b).wait_recv()
+        c_by(0, b).wait_recv()
+    gate_up(1)
     for c in dloads:
         c.wait()
 
     def product(first, rows, col):
         return jnp.dot(
-            hid_ref[pl.ds(first, rows), :], dn_ref[:, pl.ds(col, 256)],
+            hid_ref[pl.ds(first, rows), :], dn_ref[:, col:col + cut],
             preferred_element_type=jnp.float32,
         )
-
-    tiles = cut // 256
-
-    def fill(dst, dst_row, first, rows, col0):
-        @pl.loop(0, tiles)
-        def _(t):
-            off = pl.multiple_of(t * 256, 256)
-            dst[pl.ds(dst_row, rows), pl.ds(off, 256)] = product(
-                first, rows, pl.multiple_of(col0 + off, 256)
-            ).astype(dst.dtype)
-
-    def fill_acc(first, rows, col0):
-        @pl.loop(0, tiles)
-        def _(t):
-            off = pl.multiple_of(col0 + t * 256, 256)
-            acc_ref[pl.ds(first, rows), pl.ds(off, 256)] = product(first, rows, off)
 
     def block(b):
         return pl.ds(pl.multiple_of(b * tr, tr), tr)
@@ -292,18 +284,31 @@
 
     order = (3 - 3 * (z // 2), 2 * (1 - z % 2) + z // 2, 1 + z % 2, z)
 
-    fill(sa1, 0, 2 * line, 2 * line, 0)
-    for k in range(2):
+    activate(1)
+    res = product(line, 2 * line, 0)
+    sa1[0:line, :] = res[line:].astype(jnp.bfloat16)
+    acc_ref[line:2 * line, 0:cut] = res[:line]
+    for k in range(zn):
+        c_xy(0, order[k]).start()
+    res = product(line, 2 * line, cut)
+    sb1[0:line, :] = res[:line].astype(jnp.bfloat16)
+    acc_ref[2 * line:3 * line, cut:] = res[line:]
+    for k in range(zn):
+        c_xy(1, order[k]).start()
+
+    for b in range(zn):
+        c_ax(1, b).wait_recv()
+        c_by(1, b).wait_recv()
+    gate_up(2)
+    acc_ref[0:line, 0:cut] = product(0, line, 0)
+    acc_ref[0:line, cut:] = product(0, line, cut)
+    activate(2)
+    sa1[line:2 * line, :] = product(3 * line, line, 0).astype(jnp.bfloat16)
+    for k in range(zn):
         c_xy(4, order[k]).start()
-        c_xy(0, order[k]).start()
-    fill(sb1, line, 3 * line, line, cut)
-    fill(sb1, 0, line, line, cut)
-    for k in range(2):
+    sb1[line:2 * line, :] = product(3 * line, line, cut).astype(jnp.bfloat16)
+    for k in range(zn):
         c_xy(5, order[k]).start()
-        c_xy(1, order[k]).start()
-    fill_acc(0, 2 * line, 0)
-    fill_acc(2 * line, line, cut)
-    fill_acc(0, line, cut)
 
     def shifted(base, d):
         return pl.ds(pl.multiple_of(base + d * tr, tr), tr)
@@ -320,84 +325,46 @@
         ).astype(jnp.bfloat16)
         c_xy(3, d).start()
 
-    def settle(d):
-        c_xy(0, d).wait_recv()
-        c_xy(2, d).wait_recv()
-        acc_ref[block(d), 0:cut] += ra1[block(d), :].astype(jnp.float32) + ra2[
+    def c_z(h, d):
+        cols = pl.ds(h * cut, cut)
+        return pltpu.make_async_remote_copy(
+            src_ref=zsend.at[block(d), cols], dst_ref=zrecv.at[own, cols],
+            send_sem=z_send.at[h, d], recv_sem=z_recv.at[h, z],
+            device_id=at(d * 4 + y * 2 + x), device_id_type=mesh_id,
+        )
+
+    def c_zin(h, b):
+        cols = pl.ds(h * cut, cut)
+        return pltpu.make_async_remote_copy(
+            src_ref=zsend.at[block(b), cols], dst_ref=zrecv.at[block(b), cols],
+            send_sem=z_send.at[h, b], recv_sem=z_recv.at[h, b],
+            device_id=at(b * 4 + y * 2 + x), device_id_type=mesh_id,
+        )
+
+    def settled(h, d):
+        cols = slice(h * cut, (h + 1) * cut)
+        first, r1, r2 = ((0, ra1, ra2), (1, rb1, rb2))[h]
+        c_xy(first, d).wait_recv()
+        c_xy(first + 2, d).wait_recv()
+        return acc_ref[block(d), cols] + r1[block(d), :].astype(jnp.float32) + r2[
             block(d), :
         ].astype(jnp.float32)
-        c_xy(1, d).wait_recv()
-        c_xy(3, d).wait_recv()
-        acc_ref[block(d), cut:] += rb1[block(d), :].astype(jnp.float32) + rb2[
-            block(d), :
-        ].astype(jnp.float32)
-
-    def c_zr(h, d):
-        cols = pl.ds(h * cut, cut)
-        return pltpu.make_async_remote_copy(
-            src_ref=zsend.at[block(d), cols], dst_ref=zright.at[block(d), cols],
-            send_sem=z_send.at[h, d], recv_sem=zr_recv.at[h, d],
-            device_id=up, device_id_type=mesh_id,
-        )
-
-    def c_zl(h, d):
-        cols = pl.ds(h * cut, cut)
-        return pltpu.make_async_remote_copy(
-            src_ref=zsend.at[block(d), cols], dst_ref=zleft.at[block(d), cols],
-            send_sem=z_send.at[h, d], recv_sem=zl_recv.at[h, d],
-            device_id=down, device_id_type=mesh_id,
-        )
-
-    def push(h, d, make, buf, has_source):
-        cols = slice(h * cut, (h + 1) * cut)
-
-        @pl.when(has_source)
-        def _():
-            make(h, d).wait_recv()
-            zsend[block(d), cols] = (
-                acc_ref[block(d), cols] + buf[block(d), cols].astype(jnp.float32)
-            ).astype(jnp.bfloat16)
-
-        @pl.when(jnp.logical_not(has_source))
-        def _():
-            zsend[block(d), cols] = acc_ref[block(d), cols].astype(jnp.bfloat16)
-
-        make(h, d).start()
-
-    def along(d):
-        for h in range(2):
-            @pl.when(d > z)
-            def _():
-                push(h, d, c_zr, zright, z > 0)
-
-            @pl.when(d < z)
-            def _():
-                push(h, d, c_zl, zleft, z < zn - 1)
 
     for k in range(zn):
         second(order[k])
-        if k + 2 < zn:
-            for kind in (4, 0, 5, 1):
-                c_xy(kind, order[k + 2]).start()
         if k > 0:
-            settle(order[k - 1])
-            along(order[k - 1])
-    settle(z)
+            d = order[k - 1]
+            for h in range(2):
+                zsend[block(d), h * cut:(h + 1) * cut] = settled(h, d).astype(jnp.bfloat16)
+                c_z(h, d).start()
 
     for h in range(2):
         cols = slice(h * cut, (h + 1) * cut)
-
-        @pl.when(z > 0)
-        def _():
-            c_zr(h, z).wait_recv()
-            acc_ref[own, cols] += zright[own, cols].astype(jnp.float32)
-
-        @pl.when(z < zn - 1)
-        def _():
-            c_zl(h, z).wait_recv()
-            acc_ref[own, cols] += zleft[own, cols].astype(jnp.float32)
-
-        out_ref[:, cols] = acc_ref[own, cols].astype(out_ref.dtype)
+        total = settled(h, z)
+        for b in order[:zn - 1]:
+            c_zin(h, b).wait_recv()
+            total = total + zrecv[block(b), cols].astype(jnp.float32)
+        out_ref[:, cols] = total.astype(out_ref.dtype)
 
     for b in range(zn):
         for h in range(2):
@@ -414,10 +381,10 @@
         for h in range(2):
             @pl.when(b != z)
             def _():
-                c_zr(h, b).wait_send()
+                c_z(h, b).wait_send()
         for kind in range(6):
             c_xy(kind, b).wait_send()
-    for r in range(2):
+    for r in range(3):
         for i in range(4):
             c_g(r, i).wait_send()
 
@@ -438,8 +405,8 @@
     dma = pltpu.SemaphoreType.DMA
     return pl.pallas_call(
         functools.partial(layer_kernel, zn),
-        out_shape=jax.ShapeDtypeStruct((tr, half), bf),
-        in_specs=[vm, vm, vm, hbm, hbm, hbm, hbm],
+        out_shape=pltpu.VMEM((tr, half), bf),
+        in_specs=[hbm] * 7,
         out_specs=vm,
         scratch_shapes=[
             pltpu.VMEM((rows, half + META), bf),
@@ -454,9 +421,10 @@
             pltpu.VMEM((line, cut), bf), pltpu.VMEM((line, cut), bf),
             pltpu.VMEM((line, cut), bf), pltpu.VMEM((line, cut), bf),
             pltpu.VMEM((rows, half), f32),
-            pltpu.VMEM((line, half), bf), pltpu.VMEM((line, half), bf), pltpu.VMEM((line, half), bf),
-            dma((2, KCHUNKS)), dma((2,)), dma((10, zn)), dma((n,)), dma((n,)), dma((2, 4)), dma((2, 4)),
-            dma((6, zn)), dma((6, zn)), dma((2, zn)), dma((2, zn)), dma((2, zn)),
+            pltpu.VMEM((line, half), bf), pltpu.VMEM((line, half), bf),
+            pltpu.VMEM((1, tr), jnp.int32), pltpu.VMEM((1, tr), f32), dma((3,)),
+            dma((2, KCHUNKS)), dma((2,)), dma((10, zn)), dma((n,)), dma((n,)), dma((3, 4)), dma((3, 4)),
+            dma((6, zn)), dma((6, zn)), dma((2, zn)), dma((2, zn)),
         ],
         compiler_params=pltpu.CompilerParams(
             collective_id=0, has_side_effects=True, vmem_limit_bytes=56 * 2**20

time: 51 us -> 44.2 us (0.87)
  Pallas kernels: 49.3 us -> 43.4 us
  local copies, waits for them, and re-layouts: 1.53 us -> 0.64 us
    pallas_call x1, Pallas kernels: 49.3 us -> 43.4 us  [fused_local(): pl.pallas_call(functools.partial(layer_kernel, zn), out_shape=pltpu.VMEM(...]
    unnamed x1, local copies, waits for them, and re-layouts: 1.53 us -> 0.64 us
where the time goes in v1:
time: 44.2 us; the launch traced here: 44 us
  Pallas kernels  43.4 us (98%)
  local copies, waits for them, and re-layouts  0.64 us (1%)
    pallas_call x1, Pallas kernels, fused_local(): pl.pallas_call(functools.partial(layer_kernel, zn), out_shape=pltpu.VMEM(...  43.4 us

profile of v1, /device:TPU:0, one launch (start us, length us, event | category | flops | bytes accessed | tf_op | source)
XLA Modules:
  0.0 44.0 jit_solution(12381730011549809732)
XLA Ops:
  0.0 43.4 %shard_map.73 = bf16[16,2560]{1,0:T(8,128)(2,1)S(1)} custom-call(bf16[16,2560]{1,0:T(8,128)(2,1)} %tokens_ref.1, s32[1,16]{1,0:T(1,128)} %bitcast.2, f32[1,16]{1,0:T(1,128)} %bitcast.3, bf16[2560,2,512]{2,1,0:T(2,128)(2,1)} %egu_ref.1, bf16[512,2560]{1,0:T(8,128)(2,1)} %edn_ref.1, bf16[2560,2,512]{2,1,0:T(2,128)(2,1)} %sgu_ref.1, bf16[512,2560]{1,0:T(8,128)(2,1)} %sdn_ref.1), custom_call_target="tpu_custom_call" | custom-call | tf_op jit(solution)/shard_map/pallas_call | solution.py:406
  43.4 0.6 %copy.9 = bf16[16,2560]{1,0:T(8,128)(2,1)} copy(bf16[16,2560]{1,0:T(8,128)(2,1)S(1)} %shard_map.73) | data formatting | bytes 163840

commit v2 on v1

--- a/solution.py
+++ b/solution.py
@@ -16,8 +16,7 @@
     zn, tokens_ref, ids_ref, score_ref, egu_ref, edn_ref, sgu_ref, sdn_ref, out_ref,
     x_ref, raw_ref, w_ref, dn_ref, gsend_ref, grecv_ref, hid_ref,
     sa1, ra1, sb1, rb1, sa2, ra2, sb2, rb2, acc_ref, zsend, zrecv, id_v, score_v,
-    isem, wsem, dsem, ag_send, ag_recv_a, ag_recv_b, g_send, g_recv,
-    xy_send, xy_recv, z_send, z_recv,
+    isem, wsem, dsem, ag_send, ag_recv, far_recv, send, g_recv, early_recv, xy_recv, z_recv,
 ):
     tr, half = tokens_ref.shape
     hidden = edn_ref.shape[0]
@@ -102,32 +101,36 @@
 
     wide_a, wide_b = pl.ds(0, cut), pl.ds(cut, half + META - cut)
 
-    def copy(src_slot, dst_slot, cols, kind, b, recv, dev):
+    def copy(src_slot, dst_slot, cols, kind, recv, dev):
         return pltpu.make_async_remote_copy(
             src_ref=x_ref.at[rows_of(*src_slot), cols],
             dst_ref=x_ref.at[rows_of(*dst_slot), cols],
-            send_sem=ag_send.at[kind, b],
-            recv_sem=recv.at[(dst_slot[0] * 2 + dst_slot[1]) * zn + dst_slot[2]],
+            send_sem=ag_send.at[kind], recv_sem=recv,
             device_id=dev, device_id_type=mesh_id,
         )
 
     def c_up(h, b):
-        return copy((0, 0, b), (0, 0, b), (wide_a, wide_b)[h], 8 * h, b, (ag_recv_a, ag_recv_b)[h], up)
+        return copy((0, 0, b), (0, 0, b), (wide_a, wide_b)[h], 1, ag_recv.at[h, b], up)
 
     def c_down(h, b):
-        return copy((0, 0, b), (0, 0, b), (wide_a, wide_b)[h], 8 * h + 1, b, (ag_recv_a, ag_recv_b)[h], down)
+        return copy((0, 0, b), (0, 0, b), (wide_a, wide_b)[h], 2, ag_recv.at[h, b], down)
 
     def c_ay(b):
-        return copy((0, 0, b), (0, 1, b), wide_a, 2, b, ag_recv_a, yn)
+        return copy((0, 0, b), (0, 1, b), wide_a, 0, ag_recv.at[2, b], yn)
 
     def c_ax(yr, b):
-        return copy((0, yr, b), (1, yr, b), wide_a, 3 + yr, b, ag_recv_a, xn)
+        return copy((0, yr, b), (1, yr, b), wide_a, 0, far_recv.at[0, yr], xn)
 
     def c_bx(b):
-        return copy((0, 0, b), (1, 0, b), wide_b, 5, b, ag_recv_b, xn)
+        return copy((0, 0, b), (1, 0, b), wide_b, 0, ag_recv.at[3, b], xn)
 
     def c_by(xr, b):
-        return copy((xr, 0, b), (xr, 1, b), wide_b, 6 + xr, b, ag_recv_b, yn)
+        return copy((xr, 0, b), (xr, 1, b), wide_b, 0, far_recv.at[1, xr], yn)
+
+    def far_wait(kind, r):
+        rows = pl.ds((3 if r else (2, 1)[kind]) * line, line)
+        part = x_ref.at[rows, (wide_a, wide_b)[kind]]
+        pltpu.make_async_copy(part, part, far_recv.at[kind, r]).wait()
 
     def spread(h, b):
         if h == 0:
@@ -154,11 +157,9 @@
             @pl.loop(0, kc // step)
             def _(i):
                 s = pl.ds(pl.multiple_of(k * kc + i * step, step), step)
-                pair = raw_ref[m, s].reshape(step, 2 * hidden)
-                for j in range(2):
-                    for p in range(2):
-                        to = (m * 2 + j) * hidden + p * hw
-                        w_ref[s, to:to + hw] = pair[:, p * hidden + j * hw:p * hidden + (j + 1) * hw]
+                w_ref[s, m * 2 * hidden:(m + 1) * 2 * hidden] = raw_ref[m, s].reshape(
+                    step, 2 * hidden
+                )
 
     for h in range(2):
         @pl.when(z < zn - 1)
@@ -219,15 +220,15 @@
         part = pl.ds(*groups[r])
         return pltpu.make_async_remote_copy(
             src_ref=gsend_ref.at[i, part], dst_ref=grecv_ref.at[i, part],
-            send_sem=g_send.at[r, i], recv_sem=g_recv.at[r, i],
+            send_sem=send.at[0], recv_sem=g_recv.at[r, i],
             device_id=partner, device_id_type=mesh_id,
         )
 
     def gate_up(r):
         part = pl.ds(*groups[r])
-        for i in range(4):
+        for i in range(2):
             gsend_ref[i, part] = jnp.dot(
-                x_ref[part, :half], w_ref[:, i * hidden:(i + 1) * hidden],
+                x_ref[part, :half], w_ref[:, i * 2 * hidden:(i + 1) * 2 * hidden],
                 preferred_element_type=jnp.float32,
             ).astype(jnp.bfloat16)
             c_g(r, i).start()
@@ -238,13 +239,18 @@
         part = pl.ds(*groups[r])
         info = x_ref[part, half:].astype(jnp.float32)
         scale = jnp.where(info[:, 2:3] == own_expert, info[:, 0:1] + info[:, 1:2], 0.0)
-        for i in range(4):
+        for i in range(2):
             c_g(r, i).wait_recv()
-            total = gsend_ref[i, part].astype(jnp.float32) + grecv_ref[i, part].astype(jnp.float32)
-            if i < 2:
-                total = total * scale
-            g, u = total[:, :hw], total[:, hw:]
-            hid_ref[part, i * hw:(i + 1) * hw] = (g / (1.0 + jnp.exp(-g)) * u).astype(jnp.bfloat16)
+            for j in range(2):
+                g, u = (
+                    gsend_ref[i, part, c:c + hw].astype(jnp.float32)
+                    + grecv_ref[i, part, c:c + hw].astype(jnp.float32)
+                    for c in (j * hw, hidden + j * hw)
+                )
+                if i == 0:
+                    g, u = g * scale, u * scale
+                col = i * hidden + j * hw
+                hid_ref[part, col:col + hw] = (g / (1.0 + jnp.exp(-g)) * u).astype(jnp.bfloat16)
 
     gate_up(0)
 
@@ -257,16 +263,15 @@
         relay(jnp.minimum(z + zn - 1, zn - 1))
 
     activate(0)
-    for b in range(zn):
-        c_ax(0, b).wait_recv()
-        c_by(0, b).wait_recv()
+    far_wait(0, 0)
+    far_wait(1, 0)
     gate_up(1)
     for c in dloads:
         c.wait()
 
-    def product(first, rows, col):
+    def product(first, rows, col=0, width=half):
         return jnp.dot(
-            hid_ref[pl.ds(first, rows), :], dn_ref[:, col:col + cut],
+            hid_ref[pl.ds(first, rows), :], dn_ref[:, col:col + width],
             preferred_element_type=jnp.float32,
         )
 
@@ -278,36 +283,33 @@
         rows = pl.ds(pl.multiple_of((line if kind >= 4 else 0) + d * tr, tr), tr)
         return pltpu.make_async_remote_copy(
             src_ref=src.at[rows], dst_ref=dst.at[rows],
-            send_sem=xy_send.at[kind, d], recv_sem=xy_recv.at[kind, d],
+            send_sem=send.at[1],
+            recv_sem=early_recv.at[kind] if kind < 2 else xy_recv.at[kind - 2, d],
             device_id=dev, device_id_type=mesh_id,
         )
 
     order = (3 - 3 * (z // 2), 2 * (1 - z % 2) + z // 2, 1 + z % 2, z)
 
+    acc_ref[0:line, 0:cut] = product(0, line, 0, cut)
     activate(1)
-    res = product(line, 2 * line, 0)
-    sa1[0:line, :] = res[line:].astype(jnp.bfloat16)
-    acc_ref[line:2 * line, 0:cut] = res[:line]
+    res = product(line, 2 * line)
+    sa1[0:line, :] = res[line:, :cut].astype(jnp.bfloat16)
+    sb1[0:line, :] = res[:line, cut:].astype(jnp.bfloat16)
     for k in range(zn):
         c_xy(0, order[k]).start()
-    res = product(line, 2 * line, cut)
-    sb1[0:line, :] = res[:line].astype(jnp.bfloat16)
-    acc_ref[2 * line:3 * line, cut:] = res[line:]
-    for k in range(zn):
         c_xy(1, order[k]).start()
-
-    for b in range(zn):
-        c_ax(1, b).wait_recv()
-        c_by(1, b).wait_recv()
+    acc_ref[line:2 * line, 0:cut] = res[:line, :cut]
+    acc_ref[2 * line:3 * line, cut:] = res[line:, cut:]
+    far_wait(0, 1)
+    far_wait(1, 1)
     gate_up(2)
-    acc_ref[0:line, 0:cut] = product(0, line, 0)
-    acc_ref[0:line, cut:] = product(0, line, cut)
+    acc_ref[0:line, cut:] = product(0, line, cut, cut)
     activate(2)
-    sa1[line:2 * line, :] = product(3 * line, line, 0).astype(jnp.bfloat16)
+    res = product(3 * line, line).astype(jnp.bfloat16)
+    sa1[line:2 * line, :] = res[:, :cut]
+    sb1[line:2 * line, :] = res[:, cut:]
     for k in range(zn):
         c_xy(4, order[k]).start()
-    sb1[line:2 * line, :] = product(3 * line, line, cut).astype(jnp.bfloat16)
-    for k in range(zn):
         c_xy(5, order[k]).start()
 
     def shifted(base, d):
@@ -329,22 +331,16 @@
         cols = pl.ds(h * cut, cut)
         return pltpu.make_async_remote_copy(
             src_ref=zsend.at[block(d), cols], dst_ref=zrecv.at[own, cols],
-            send_sem=z_send.at[h, d], recv_sem=z_recv.at[h, z],
+            send_sem=send.at[2], recv_sem=z_recv.at[h],
             device_id=at(d * 4 + y * 2 + x), device_id_type=mesh_id,
         )
 
-    def c_zin(h, b):
-        cols = pl.ds(h * cut, cut)
-        return pltpu.make_async_remote_copy(
-            src_ref=zsend.at[block(b), cols], dst_ref=zrecv.at[block(b), cols],
-            send_sem=z_send.at[h, b], recv_sem=z_recv.at[h, b],
-            device_id=at(b * 4 + y * 2 + x), device_id_type=mesh_id,
-        )
+    def arrived(sem, part):
+        pltpu.make_async_copy(part, part, sem).wait()
 
     def settled(h, d):
         cols = slice(h * cut, (h + 1) * cut)
         first, r1, r2 = ((0, ra1, ra2), (1, rb1, rb2))[h]
-        c_xy(first, d).wait_recv()
         c_xy(first + 2, d).wait_recv()
         return acc_ref[block(d), cols] + r1[block(d), :].astype(jnp.float32) + r2[
             block(d), :
@@ -352,41 +348,41 @@
 
     for k in range(zn):
         second(order[k])
-        if k > 0:
-            d = order[k - 1]
-            for h in range(2):
-                zsend[block(d), h * cut:(h + 1) * cut] = settled(h, d).astype(jnp.bfloat16)
-                c_z(h, d).start()
+    arrived(early_recv.at[0], ra1.at[pl.ds(0, line)])
+    arrived(early_recv.at[1], rb1.at[pl.ds(0, line)])
+    for k in range(zn - 1):
+        d = order[k]
+        for h in range(2):
+            zsend[block(d), h * cut:(h + 1) * cut] = settled(h, d).astype(jnp.bfloat16)
+            c_z(h, d).start()
 
     for h in range(2):
         cols = slice(h * cut, (h + 1) * cut)
         total = settled(h, z)
+        arrived(z_recv.at[h], zrecv.at[pl.ds(0, line - tr), pl.ds(h * cut, cut)])
         for b in order[:zn - 1]:
-            c_zin(h, b).wait_recv()
             total = total + zrecv[block(b), cols].astype(jnp.float32)
         out_ref[:, cols] = total.astype(out_ref.dtype)
 
+    def sent(sem, part):
+        pltpu.make_async_remote_copy(
+            src_ref=part, dst_ref=part, send_sem=sem, recv_sem=z_recv.at[0],
+            device_id=partner, device_id_type=mesh_id,
+        ).wait_send()
+
     for b in range(zn):
-        for h in range(2):
-            @pl.when(jnp.logical_and(z < zn - 1, b <= z))
-            def _():
-                c_up(h, b).wait_send()
-
-            @pl.when(jnp.logical_and(z > 0, b >= z))
-            def _():
-                c_down(h, b).wait_send()
-
-        for c in (c_ay(b), c_ax(0, b), c_ax(1, b), c_bx(b), c_by(0, b), c_by(1, b)):
-            c.wait_send()
-        for h in range(2):
-            @pl.when(b != z)
-            def _():
-                c_z(h, b).wait_send()
-        for kind in range(6):
-            c_xy(kind, b).wait_send()
-    for r in range(3):
-        for i in range(4):
-            c_g(r, i).wait_send()
+        @pl.when(jnp.logical_and(z < zn - 1, b == z))
+        def _():
+            sent(ag_send.at[1], x_ref.at[pl.ds(0, (b + 1) * tr)])
+
+        @pl.when(jnp.logical_and(z > 0, b == z))
+        def _():
+            sent(ag_send.at[2], x_ref.at[pl.ds(0, (zn - b) * tr)])
+
+    sent(ag_send.at[0], x_ref.at[pl.ds(0, 3 * line)])
+    sent(send.at[0], gsend_ref)
+    sent(send.at[1], x_ref.at[pl.ds(0, 3 * line), pl.ds(0, half)])
+    sent(send.at[2], zsend.at[pl.ds(0, line - tr)])
 
 
 def fused_local(
@@ -413,8 +409,8 @@
             pltpu.VMEM((2, half, 2, hidden), bf),
             pltpu.VMEM((half, 4 * hidden), bf),
             pltpu.VMEM((2 * hidden, half), bf),
-            pltpu.VMEM((4, rows, hidden), bf),
-            pltpu.VMEM((4, rows, hidden), bf),
+            pltpu.VMEM((2, rows, 2 * hidden), bf),
+            pltpu.VMEM((2, rows, 2 * hidden), bf),
             pltpu.VMEM((rows, 2 * hidden), bf),
             pltpu.VMEM((2 * line, cut), bf), pltpu.VMEM((2 * line, cut), bf),
             pltpu.VMEM((2 * line, cut), bf), pltpu.VMEM((2 * line, cut), bf),
@@ -423,8 +419,8 @@
             pltpu.VMEM((rows, half), f32),
             pltpu.VMEM((line, half), bf), pltpu.VMEM((line, half), bf),
             pltpu.VMEM((1, tr), jnp.int32), pltpu.VMEM((1, tr), f32), dma((3,)),
-            dma((2, KCHUNKS)), dma((2,)), dma((10, zn)), dma((n,)), dma((n,)), dma((3, 4)), dma((3, 4)),
-            dma((6, zn)), dma((6, zn)), dma((2, zn)), dma((2, zn)),
+            dma((2, KCHUNKS)), dma((2,)), dma((3,)), dma((4, zn)), dma((2, 2)), dma((3,)), dma((3, 2)),
+            dma((2,)), dma((4, zn)), dma((2,)),
         ],
         compiler_params=pltpu.CompilerParams(
             collective_id=0, has_side_effects=True, vmem_limit_bytes=56 * 2**20

time: 44.2 us -> 42.7 us (0.966)
  Pallas kernels: 43.4 us -> 41.9 us
    pallas_call x1, Pallas kernels: 43.4 us -> 41.9 us  [fused_local(): pl.pallas_call(functools.partial(layer_kernel, zn), out_shape=pltpu.VMEM(...]
where the time goes in v2:
time: 42.7 us; the launch traced here: 42.6 us
  Pallas kernels  41.9 us (98%)
  local copies, waits for them, and re-layouts  0.64 us (1%)
    pallas_call x1, Pallas kernels, fused_local(): pl.pallas_call(functools.partial(layer_kernel, zn), out_shape=pltpu.VMEM(...  41.9 us

profile of v2, /device:TPU:0, one launch (start us, length us, event | category | flops | bytes accessed | tf_op | source)
XLA Modules:
  0.0 42.6 jit_solution(12364719282949198857)
XLA Ops:
  0.0 41.9 %shard_map.73 = bf16[16,2560]{1,0:T(8,128)(2,1)S(1)} custom-call(bf16[16,2560]{1,0:T(8,128)(2,1)} %tokens_ref.1, s32[1,16]{1,0:T(1,128)} %bitcast.2, f32[1,16]{1,0:T(1,128)} %bitcast.3, bf16[2560,2,512]{2,1,0:T(2,128)(2,1)} %egu_ref.1, bf16[512,2560]{1,0:T(8,128)(2,1)} %edn_ref.1, bf16[2560,2,512]{2,1,0:T(2,128)(2,1)} %sgu_ref.1, bf16[512,2560]{1,0:T(8,128)(2,1)} %sdn_ref.1), custom_call_target="tpu_custom_call" | custom-call | tf_op jit(solution)/shard_map/pallas_call | solution.py:402
  41.9 0.6 %copy.9 = bf16[16,2560]{1,0:T(8,128)(2,1)} copy(bf16[16,2560]{1,0:T(8,128)(2,1)S(1)} %shard_map.73) | data formatting | bytes 163840

commit v3 on v2

--- a/solution.py
+++ b/solution.py
@@ -15,14 +15,16 @@
 def layer_kernel(
     zn, tokens_ref, ids_ref, score_ref, egu_ref, edn_ref, sgu_ref, sdn_ref, out_ref,
     x_ref, raw_ref, w_ref, dn_ref, gsend_ref, grecv_ref, hid_ref,
-    sa1, ra1, sb1, rb1, sa2, ra2, sb2, rb2, acc_ref, zsend, zrecv, id_v, score_v,
-    isem, wsem, dsem, ag_send, ag_recv, far_recv, send, g_recv, early_recv, xy_recv, z_recv,
+    sa1, ra1, sb1, rb1, sa2, ra2, sb2, rb2, acc_ref, zsend, zrecv, cs, cr, ps, pr, id_v, score_v,
+    isem, wsem, dsem, ag_send, ag_recv, far_recv, send, g_recv, early_recv, xy_recv, z_recv, c_recv, p_recv,
 ):
     tr, half = tokens_ref.shape
     hidden = edn_ref.shape[0]
     line = zn * tr
     hw = hidden // 2
     cut = half // 2
+    third = sa1.shape[1]
+    both = 2 * third
     kc = half // KCHUNKS
     rep = lax.axis_index("rep")
     sub = lax.axis_index("sub")
@@ -38,6 +40,7 @@
     yn = at(z * 4 + (1 - y) * 2 + x)
     up = at(jnp.minimum(z + 1, zn - 1) * 4 + y * 2 + x)
     down = at(jnp.maximum(z - 1, 0) * 4 + y * 2 + x)
+    diag = at(z * 4 + (1 - y) * 2 + (1 - x))
     partner = at(me, 1 - sub)
     mesh_id = pl.DeviceIdType.MESH
 
@@ -290,27 +293,48 @@
 
     order = (3 - 3 * (z // 2), 2 * (1 - z % 2) + z // 2, 1 + z % 2, z)
 
-    acc_ref[0:line, 0:cut] = product(0, line, 0, cut)
+    def arrived(sem, part):
+        pltpu.make_async_copy(part, part, sem).wait()
+
+    def c_c(first, count, d):
+        return pltpu.make_async_remote_copy(
+            src_ref=cs.at[pl.ds(first, count), d], dst_ref=cr.at[z, pl.ds(first, count)],
+            send_sem=send.at[3], recv_sem=c_recv.at[first],
+            device_id=at(d * 4 + y * 2 + x), device_id_type=mesh_id,
+        )
+
+    def along(first, count, res):
+        rows = slice(first * line, (first + count) * line)
+        acc_ref[rows, both:] = res
+        cs[first:first + count] = res.astype(jnp.bfloat16).reshape(count, zn, tr, half - both)
+        for d in order[:zn - 1]:
+            c_c(first, count, d).start()
+
+    res = product(0, line, third, half - third)
+    along(0, 1, res[:, third:])
+    acc_ref[0:line, third:both] = res[:, :third]
     activate(1)
     res = product(line, 2 * line)
-    sa1[0:line, :] = res[line:, :cut].astype(jnp.bfloat16)
-    sb1[0:line, :] = res[:line, cut:].astype(jnp.bfloat16)
+    sa1[0:line, :] = res[line:, :third].astype(jnp.bfloat16)
+    sb1[0:line, :] = res[:line, third:both].astype(jnp.bfloat16)
     for k in range(zn):
         c_xy(0, order[k]).start()
         c_xy(1, order[k]).start()
-    acc_ref[line:2 * line, 0:cut] = res[:line, :cut]
-    acc_ref[2 * line:3 * line, cut:] = res[line:, cut:]
+    along(1, 2, res[:, both:])
+    acc_ref[line:2 * line, 0:third] = res[:line, :third]
+    acc_ref[2 * line:3 * line, third:both] = res[line:, third:both]
     far_wait(0, 1)
     far_wait(1, 1)
     gate_up(2)
-    acc_ref[0:line, cut:] = product(0, line, cut, cut)
+    acc_ref[0:line, 0:third] = product(0, line, 0, third)
     activate(2)
-    res = product(3 * line, line).astype(jnp.bfloat16)
-    sa1[line:2 * line, :] = res[:, :cut]
-    sb1[line:2 * line, :] = res[:, cut:]
+    res = product(3 * line, line)
+    sa1[line:2 * line, :] = res[:, :third].astype(jnp.bfloat16)
+    sb1[line:2 * line, :] = res[:, third:both].astype(jnp.bfloat16)
     for k in range(zn):
         c_xy(4, order[k]).start()
         c_xy(5, order[k]).start()
+    along(3, 1, res[:, both:])
 
     def shifted(base, d):
         return pl.ds(pl.multiple_of(base + d * tr, tr), tr)
@@ -318,28 +342,38 @@
     def second(d):
         c_xy(4, d).wait_recv()
         sa2[block(d), :] = (
-            acc_ref[shifted(line, d), 0:cut] + ra1[shifted(line, d), :].astype(jnp.float32)
+            acc_ref[shifted(line, d), 0:third] + ra1[shifted(line, d), :].astype(jnp.float32)
         ).astype(jnp.bfloat16)
         c_xy(2, d).start()
         c_xy(5, d).wait_recv()
         sb2[block(d), :] = (
-            acc_ref[shifted(2 * line, d), cut:] + rb1[shifted(line, d), :].astype(jnp.float32)
+            acc_ref[shifted(2 * line, d), third:both] + rb1[shifted(line, d), :].astype(jnp.float32)
         ).astype(jnp.bfloat16)
         c_xy(3, d).start()
 
     def c_z(h, d):
-        cols = pl.ds(h * cut, cut)
+        cols = pl.ds(h * third, third)
         return pltpu.make_async_remote_copy(
             src_ref=zsend.at[block(d), cols], dst_ref=zrecv.at[own, cols],
             send_sem=send.at[2], recv_sem=z_recv.at[h],
             device_id=at(d * 4 + y * 2 + x), device_id_type=mesh_id,
         )
 
-    def arrived(sem, part):
-        pltpu.make_async_copy(part, part, sem).wait()
+    def summed(c):
+        total = acc_ref[shifted(c * line, z), both:]
+        for b in order[:zn - 1]:
+            total = total + cr[b, c].astype(jnp.float32)
+        return total
+
+    def c_p(c):
+        return pltpu.make_async_remote_copy(
+            src_ref=ps.at[c - 1], dst_ref=pr.at[c - 1],
+            send_sem=send.at[4], recv_sem=p_recv.at[0],
+            device_id=(yn, xn, diag)[c - 1], device_id_type=mesh_id,
+        )
 
     def settled(h, d):
-        cols = slice(h * cut, (h + 1) * cut)
+        cols = slice(h * third, (h + 1) * third)
         first, r1, r2 = ((0, ra1, ra2), (1, rb1, rb2))[h]
         c_xy(first + 2, d).wait_recv()
         return acc_ref[block(d), cols] + r1[block(d), :].astype(jnp.float32) + r2[
@@ -348,18 +382,28 @@
 
     for k in range(zn):
         second(order[k])
+    for first, count in ((0, 1), (1, 2), (3, 1)):
+        arrived(c_recv.at[first], cr.at[pl.ds(0, zn - 1), pl.ds(0, count)])
+    for c in (1, 2, 3):
+        ps[c - 1] = summed(c).astype(jnp.bfloat16)
+        c_p(c).start()
     arrived(early_recv.at[0], ra1.at[pl.ds(0, line)])
     arrived(early_recv.at[1], rb1.at[pl.ds(0, line)])
     for k in range(zn - 1):
         d = order[k]
         for h in range(2):
-            zsend[block(d), h * cut:(h + 1) * cut] = settled(h, d).astype(jnp.bfloat16)
+            zsend[block(d), h * third:(h + 1) * third] = settled(h, d).astype(jnp.bfloat16)
             c_z(h, d).start()
 
+    total = summed(0)
+    arrived(p_recv.at[0], pr)
+    for c in range(3):
+        total = total + pr[c].astype(jnp.float32)
+    out_ref[:, both:] = total.astype(out_ref.dtype)
     for h in range(2):
-        cols = slice(h * cut, (h + 1) * cut)
+        cols = slice(h * third, (h + 1) * third)
         total = settled(h, z)
-        arrived(z_recv.at[h], zrecv.at[pl.ds(0, line - tr), pl.ds(h * cut, cut)])
+        arrived(z_recv.at[h], zrecv.at[pl.ds(0, line - tr), pl.ds(h * third, third)])
         for b in order[:zn - 1]:
             total = total + zrecv[block(b), cols].astype(jnp.float32)
         out_ref[:, cols] = total.astype(out_ref.dtype)
@@ -381,7 +425,9 @@
 
     sent(ag_send.at[0], x_ref.at[pl.ds(0, 3 * line)])
     sent(send.at[0], gsend_ref)
-    sent(send.at[1], x_ref.at[pl.ds(0, 3 * line), pl.ds(0, half)])
+    sent(send.at[1], x_ref.at[pl.ds(0, 3 * line), pl.ds(0, both)])
+    sent(send.at[3], cs.at[pl.ds(0, zn - 1)])
+    sent(send.at[4], ps)
     sent(send.at[2], zsend.at[pl.ds(0, line - tr)])
 
 
@@ -394,7 +440,7 @@
     hidden = expert_down.shape[0]
     rows = n * tr
     line = zn * tr
-    cut = half // 2
+    third = half * 7 // 20 // 128 * 128
     bf, f32 = jnp.bfloat16, jnp.float32
     vm = pl.BlockSpec(memory_space=pltpu.VMEM)
     hbm = pl.BlockSpec(memory_space=pltpu.HBM)
@@ -412,15 +458,17 @@
             pltpu.VMEM((2, rows, 2 * hidden), bf),
             pltpu.VMEM((2, rows, 2 * hidden), bf),
             pltpu.VMEM((rows, 2 * hidden), bf),
-            pltpu.VMEM((2 * line, cut), bf), pltpu.VMEM((2 * line, cut), bf),
-            pltpu.VMEM((2 * line, cut), bf), pltpu.VMEM((2 * line, cut), bf),
-            pltpu.VMEM((line, cut), bf), pltpu.VMEM((line, cut), bf),
-            pltpu.VMEM((line, cut), bf), pltpu.VMEM((line, cut), bf),
+            pltpu.VMEM((2 * line, third), bf), pltpu.VMEM((2 * line, third), bf),
+            pltpu.VMEM((2 * line, third), bf), pltpu.VMEM((2 * line, third), bf),
+            pltpu.VMEM((line, third), bf), pltpu.VMEM((line, third), bf),
+            pltpu.VMEM((line, third), bf), pltpu.VMEM((line, third), bf),
             pltpu.VMEM((rows, half), f32),
-            pltpu.VMEM((line, half), bf), pltpu.VMEM((line, half), bf),
+            pltpu.VMEM((line, 2 * third), bf), pltpu.VMEM((line, 2 * third), bf),
+            pltpu.VMEM((4, zn, tr, half - 2 * third), bf), pltpu.VMEM((zn, 4, tr, half - 2 * third), bf),
+            pltpu.VMEM((3, tr, half - 2 * third), bf), pltpu.VMEM((3, tr, half - 2 * third), bf),
             pltpu.VMEM((1, tr), jnp.int32), pltpu.VMEM((1, tr), f32), dma((3,)),
-            dma((2, KCHUNKS)), dma((2,)), dma((3,)), dma((4, zn)), dma((2, 2)), dma((3,)), dma((3, 2)),
-            dma((2,)), dma((4, zn)), dma((2,)),
+            dma((2, KCHUNKS)), dma((2,)), dma((3,)), dma((4, zn)), dma((2, 2)), dma((5,)), dma((3, 2)),
+            dma((2,)), dma((4, zn)), dma((2,)), dma((4,)), dma((1,)),
         ],
         compiler_params=pltpu.CompilerParams(
             collective_id=0, has_side_effects=True, vmem_limit_bytes=56 * 2**20

time: 42.7 us -> 39.9 us (0.934)
  Pallas kernels: 41.9 us -> 39.1 us
    pallas_call x1, Pallas kernels: 41.9 us -> 39.1 us  [fused_local(): pl.pallas_call(functools.partial(layer_kernel, zn), out_shape=pltpu.VMEM(...]
where the time goes in v3:
time: 39.9 us; the launch traced here: 39.7 us
  Pallas kernels  39.1 us (98%)
  local copies, waits for them, and re-layouts  0.64 us (2%)
    pallas_call x1, Pallas kernels, fused_local(): pl.pallas_call(functools.partial(layer_kernel, zn), out_shape=pltpu.VMEM(...  39.1 us

profile of v3, /device:TPU:0, one launch (start us, length us, event | category | flops | bytes accessed | tf_op | source)
XLA Modules:
  0.0 39.7 jit_solution(10131451740230519439)
XLA Ops:
  0.0 39.1 %shard_map.73 = bf16[16,2560]{1,0:T(8,128)(2,1)S(1)} custom-call(bf16[16,2560]{1,0:T(8,128)(2,1)} %tokens_ref.1, s32[1,16]{1,0:T(1,128)} %bitcast.2, f32[1,16]{1,0:T(1,128)} %bitcast.3, bf16[2560,2,512]{2,1,0:T(2,128)(2,1)} %egu_ref.1, bf16[512,2560]{1,0:T(8,128)(2,1)} %edn_ref.1, bf16[2560,2,512]{2,1,0:T(2,128)(2,1)} %sgu_ref.1, bf16[512,2560]{1,0:T(8,128)(2,1)} %sdn_ref.1), custom_call_target="tpu_custom_call" | custom-call | tf_op jit(solution)/shard_map/pallas_call | solution.py:448
  39.1 0.6 %copy.9 = bf16[16,2560]{1,0:T(8,128)(2,1)} copy(bf16[16,2560]{1,0:T(8,128)(2,1)S(1)} %shard_map.73) | data formatting | bytes 163840

commit v4 on v3

--- a/solution.py
+++ b/solution.py
@@ -103,6 +103,11 @@
         return pl.ds(pl.multiple_of(((xr * 2 + yr) * zn + b) * tr, tr), tr)
 
     wide_a, wide_b = pl.ds(0, cut), pl.ds(cut, half + META - cut)
+    piece_w = cut // 2 // 128 * 128
+    parts = (
+        pl.ds(0, piece_w), pl.ds(piece_w, cut - piece_w),
+        pl.ds(cut, piece_w), pl.ds(cut + piece_w, half + META - cut - piece_w),
+    )
 
     def copy(src_slot, dst_slot, cols, kind, recv, dev):
         return pltpu.make_async_remote_copy(
@@ -113,19 +118,19 @@
         )
 
     def c_up(h, b):
-        return copy((0, 0, b), (0, 0, b), (wide_a, wide_b)[h], 1, ag_recv.at[h, b], up)
+        return copy((0, 0, b), (0, 0, b), parts[h], 1, ag_recv.at[h, b], up)
 
     def c_down(h, b):
-        return copy((0, 0, b), (0, 0, b), (wide_a, wide_b)[h], 2, ag_recv.at[h, b], down)
+        return copy((0, 0, b), (0, 0, b), parts[h], 2, ag_recv.at[h, b], down)
 
     def c_ay(b):
-        return copy((0, 0, b), (0, 1, b), wide_a, 0, ag_recv.at[2, b], yn)
+        return copy((0, 0, b), (0, 1, b), wide_a, 0, ag_recv.at[4, b], yn)
 
     def c_ax(yr, b):
         return copy((0, yr, b), (1, yr, b), wide_a, 0, far_recv.at[0, yr], xn)
 
     def c_bx(b):
-        return copy((0, 0, b), (1, 0, b), wide_b, 0, ag_recv.at[3, b], xn)
+        return copy((0, 0, b), (1, 0, b), wide_b, 0, ag_recv.at[5, b], xn)
 
     def c_by(xr, b):
         return copy((xr, 0, b), (xr, 1, b), wide_b, 0, far_recv.at[1, xr], yn)
@@ -164,7 +169,7 @@
                     step, 2 * hidden
                 )
 
-    for h in range(2):
+    for h in range(4):
         @pl.when(z < zn - 1)
         def _():
             c_up(h, z).start()
@@ -179,7 +184,7 @@
     c_by(0, z).start()
     deinterleave(4)
     for s in range(1, zn):
-        for h in range(2):
+        for h in range(4):
             @pl.when(z - s >= 0)
             def _():
                 b = jnp.maximum(z - s, 0)
@@ -189,7 +194,8 @@
                 def _():
                     c_up(h, b).start()
 
-                spread(h, b)
+                if h % 2:
+                    spread(h // 2, b)
 
             @pl.when(z + s <= zn - 1)
             def _():
@@ -200,7 +206,8 @@
                 def _():
                     c_down(h, b).start()
 
-                spread(h, b)
+                if h % 2:
+                    spread(h // 2, b)
 
         if s == 1:
             relay(z)
@@ -230,51 +237,43 @@
     def gate_up(r):
         part = pl.ds(*groups[r])
         for i in range(2):
+            lead = line if r == 2 else 0
+            rows = pl.ds(groups[r][0] - lead, groups[r][1] + lead)
             gsend_ref[i, part] = jnp.dot(
-                x_ref[part, :half], w_ref[:, i * 2 * hidden:(i + 1) * 2 * hidden],
+                x_ref[rows, :half], w_ref[:, i * 2 * hidden:(i + 1) * 2 * hidden],
                 preferred_element_type=jnp.float32,
-            ).astype(jnp.bfloat16)
+            )[lead:].astype(jnp.bfloat16)
             c_g(r, i).start()
 
     own_expert = (me // EXP_ROWS).astype(jnp.float32)
 
-    def activate(r):
+    def activate(r, i):
         part = pl.ds(*groups[r])
-        info = x_ref[part, half:].astype(jnp.float32)
-        scale = jnp.where(info[:, 2:3] == own_expert, info[:, 0:1] + info[:, 1:2], 0.0)
-        for i in range(2):
-            c_g(r, i).wait_recv()
-            for j in range(2):
-                g, u = (
-                    gsend_ref[i, part, c:c + hw].astype(jnp.float32)
-                    + grecv_ref[i, part, c:c + hw].astype(jnp.float32)
-                    for c in (j * hw, hidden + j * hw)
-                )
-                if i == 0:
-                    g, u = g * scale, u * scale
-                col = i * hidden + j * hw
-                hid_ref[part, col:col + hw] = (g / (1.0 + jnp.exp(-g)) * u).astype(jnp.bfloat16)
-
-    gate_up(0)
-
-    @pl.when(z - zn + 1 >= 0)
-    def _():
-        relay(jnp.maximum(z - zn + 1, 0))
-
-    @pl.when(z + zn - 1 <= zn - 1)
-    def _():
-        relay(jnp.minimum(z + zn - 1, zn - 1))
-
-    activate(0)
-    far_wait(0, 0)
-    far_wait(1, 0)
-    gate_up(1)
-    for c in dloads:
-        c.wait()
-
-    def product(first, rows, col=0, width=half):
+        if i == 0:
+            info = x_ref[part, half:].astype(jnp.float32)
+            scale = jnp.where(info[:, 2:3] == own_expert, info[:, 0:1] + info[:, 1:2], 0.0)
+        c_g(r, i).wait_recv()
+        for j in range(2):
+            g, u = (
+                gsend_ref[i, part, c:c + hw].astype(jnp.float32)
+                + grecv_ref[i, part, c:c + hw].astype(jnp.float32)
+                for c in (j * hw, hidden + j * hw)
+            )
+            if i == 0:
+                g, u = g * scale, u * scale
+            col = i * hidden + j * hw
+            hid_ref[part, col:col + hw] = (g / (1.0 + jnp.exp(-g)) * u).astype(jnp.bfloat16)
+
+    def product(first, rows, col, width):
         return jnp.dot(
             hid_ref[pl.ds(first, rows), :], dn_ref[:, col:col + width],
+            preferred_element_type=jnp.float32,
+        )
+
+    def piece(r, i):
+        units = slice(i * hidden, (i + 1) * hidden)
+        return jnp.dot(
+            hid_ref[pl.ds(*groups[r]), units], dn_ref[units, :],
             preferred_element_type=jnp.float32,
         )
 
@@ -310,11 +309,27 @@
         for d in order[:zn - 1]:
             c_c(first, count, d).start()
 
-    res = product(0, line, third, half - third)
-    along(0, 1, res[:, third:])
-    acc_ref[0:line, third:both] = res[:, :third]
-    activate(1)
-    res = product(line, 2 * line)
+    gate_up(0)
+    activate(0, 0)
+    activate(0, 1)
+    for c in dloads:
+        c.wait()
+    along(0, 1, product(0, line, both, half - both))
+    @pl.when(z - zn + 1 >= 0)
+    def _():
+        relay(jnp.maximum(z - zn + 1, 0))
+
+    @pl.when(z + zn - 1 <= zn - 1)
+    def _():
+        relay(jnp.minimum(z + zn - 1, zn - 1))
+
+    far_wait(0, 0)
+    far_wait(1, 0)
+    gate_up(1)
+    activate(1, 0)
+    acc_ref[line:3 * line, :] = piece(1, 0)
+    activate(1, 1)
+    res = acc_ref[line:3 * line, :] + piece(1, 1)
     sa1[0:line, :] = res[line:, :third].astype(jnp.bfloat16)
     sb1[0:line, :] = res[:line, third:both].astype(jnp.bfloat16)
     for k in range(zn):
@@ -326,15 +341,17 @@
     far_wait(0, 1)
     far_wait(1, 1)
     gate_up(2)
-    acc_ref[0:line, 0:third] = product(0, line, 0, third)
-    activate(2)
-    res = product(3 * line, line)
+    activate(2, 0)
+    acc_ref[3 * line:, :] = piece(2, 0)
+    activate(2, 1)
+    res = acc_ref[3 * line:, :] + piece(2, 1)
+    along(3, 1, res[:, both:])
     sa1[line:2 * line, :] = res[:, :third].astype(jnp.bfloat16)
     sb1[line:2 * line, :] = res[:, third:both].astype(jnp.bfloat16)
     for k in range(zn):
         c_xy(4, order[k]).start()
         c_xy(5, order[k]).start()
-    along(3, 1, res[:, both:])
+    acc_ref[0:line, 0:both] = product(0, line, 0, both)
 
     def shifted(base, d):
         return pl.ds(pl.multiple_of(base + d * tr, tr), tr)
@@ -440,7 +457,7 @@
     hidden = expert_down.shape[0]
     rows = n * tr
     line = zn * tr
-    third = half * 7 // 20 // 128 * 128
+    third = half * 6 // 20 // 128 * 128
     bf, f32 = jnp.bfloat16, jnp.float32
     vm = pl.BlockSpec(memory_space=pltpu.VMEM)
     hbm = pl.BlockSpec(memory_space=pltpu.HBM)
@@ -467,7 +484,7 @@
             pltpu.VMEM((4, zn, tr, half - 2 * third), bf), pltpu.VMEM((zn, 4, tr, half - 2 * third), bf),
             pltpu.VMEM((3, tr, half - 2 * third), bf), pltpu.VMEM((3, tr, half - 2 * third), bf),
             pltpu.VMEM((1, tr), jnp.int32), pltpu.VMEM((1, tr), f32), dma((3,)),
-            dma((2, KCHUNKS)), dma((2,)), dma((3,)), dma((4, zn)), dma((2, 2)), dma((5,)), dma((3, 2)),
+            dma((2, KCHUNKS)), dma((2,)), dma((3,)), dma((6, zn)), dma((2, 2)), dma((5,)), dma((3, 2)),
             dma((2,)), dma((4, zn)), dma((2,)), dma((4,)), dma((1,)),
         ],
         compiler_params=pltpu.CompilerParams(

time: 39.9 us -> 39.8 us (level)
  no operation moved by 1% of the time
where the time goes in v4:
time: 39.8 us; the launch traced here: 39.6 us
  Pallas kernels  39 us (98%)
  local copies, waits for them, and re-layouts  0.64 us (2%)
    pallas_call x1, Pallas kernels, fused_local(): pl.pallas_call(functools.partial(layer_kernel, zn), out_shape=pltpu.VMEM(...  39 us

profile of v4, /device:TPU:0, one launch (start us, length us, event | category | flops | bytes accessed | tf_op | source)
XLA Modules:
  0.0 39.6 jit_solution(1794262619778017674)
XLA Ops:
  0.0 39.0 %shard_map.73 = bf16[16,2560]{1,0:T(8,128)(2,1)S(1)} custom-call(bf16[16,2560]{1,0:T(8,128)(2,1)} %tokens_ref.1, s32[1,16]{1,0:T(1,128)} %bitcast.2, f32[1,16]{1,0:T(1,128)} %bitcast.3, bf16[2560,2,512]{2,1,0:T(2,128)(2,1)} %egu_ref.1, bf16[512,2560]{1,0:T(8,128)(2,1)} %edn_ref.1, bf16[2560,2,512]{2,1,0:T(2,128)(2,1)} %sgu_ref.1, bf16[512,2560]{1,0:T(8,128)(2,1)} %sdn_ref.1), custom_call_target="tpu_custom_call" | custom-call | tf_op jit(solution)/shard_map/pallas_call | solution.py:465
  39.0 0.6 %copy.9 = bf16[16,2560]{1,0:T(8,128)(2,1)} copy(bf16[16,2560]{1,0:T(8,128)(2,1)S(1)} %shard_map.73) | data formatting | bytes 163840
